TPU v7x, 32 devices: a whole 2x2x4 slice. The times are simulated.
32 devices in a mesh: node: 8 (over z, core), group: 4 (over y, x).
Axes of the slice: x: 2, y: 2, z: 4, core: 2. Of those that a mesh axis runs over, the one named last changes fastest.
Arguments:
- gradient: bfloat16 [8, 4, 128, 1024], P('node', 'group'), may hold values from -60 to 60
- momentum: float32 [128, 1024], replicated, may hold values from -6 to 6
- variance: float32 [128, 1024], replicated, may hold values from 0.004 to 0.4
- params: float32 [128, 1024], replicated, may hold values from -6 to 6
- worker_error: float32 [8, 4, 128, 1024], P('node', 'group'), may hold values from -18 to 18, as said below
- server_error: float32 [4, 128, 1024], P('group', 'node'), may hold values from -12 to 12, as said below
- group_worker_error: float32 [4, 128, 1024], P('group', 'node'), may hold values from -12 to 12, as said below
- group_server_error: float32 [128, 1024], P(('node', 'group')), may hold values from -12 to 12, as said below
Outputs:
- new_params: float32 [128, 1024], replicated
- new_momentum: float32 [128, 1024], replicated
- new_worker_error: float32 [8, 4, 128, 1024], P('node', 'group')
- new_server_error: float32 [4, 128, 1024], P('group', 'node')
- new_group_worker_error: float32 [4, 128, 1024], P('group', 'node')
- new_group_server_error: float32 [128, 1024], P(('node', 'group'))
Inputs may be any that keep to these rules, and one draw needn't show every extreme that they name: `worker_error`: no entry of local has magnitude under 0.005. No entry of group_mean + server_error has magnitude under 0.005. No entry of group_q + group_worker_error has magnitude under 0.005. No entry of total_mean + group_server_error has magnitude under 0.005.
All inputs are finite; a program needn't handle non-finite values.
Results may differ from a plain program's by a relative error of at most 0.0003.
Values sent between devices are 32-bit elements; how exact they have to be, the bound alone decides.
No kernel may reach another device: no remote copies, remote signals or barrier semaphores. Data moves between devices by JAX's collectives and lax.ppermute only.
A program may use at most 128 MiB of HBM per device.

v0:
```python
import functools

import jax
import jax.numpy as jnp
from jax import lax
from jax.experimental import pallas as pl
from jax.experimental.pallas import tpu as pltpu
from jax.sharding import PartitionSpec as P

CORES = 2
VMEM = pl.BlockSpec(memory_space=pltpu.VMEM)
HBM = pl.BlockSpec(memory_space=pltpu.HBM)


def paired(size):
    return size & (size - 1) == 0


def target(index, step, size):
    if paired(size):
        return index ^ step
    return lax.rem(index + step, size) if not isinstance(index, int) else (index + step) % size


def source(index, step, size):
    return index ^ step if paired(size) else lax.rem(index + (size - step), size)


def farthest_first(size):
    return list(range(size - 1, 0, -1))


def farthest_last(size):
    steps = farthest_first(size)
    return steps[1:] + steps[:1]


def crossed_back(step):
    return step > 0 and step % 2 == 0


def packed_of(values, width):
    scale = jnp.sum(jnp.abs(values), axis=-1, keepdims=True) / width
    return jnp.where(values > 0, scale, jnp.where(values < 0, -scale, jnp.zeros_like(values)))


def swap_cores(values, nodes):
    return lax.ppermute(values, "node", [(i, i ^ 1) for i in range(nodes)])


def send_chip(values, step, nodes, crossed):
    chips = nodes // CORES
    pairs = [
        (CORES * i + core, CORES * target(i, step, chips) + (1 - core if crossed else core))
        for i in range(chips)
        for core in range(CORES)
    ]
    return lax.ppermute(values, "node", pairs)


def send_group(values, steps, nodes, groups):
    pairs = [
        (i * groups + j, i * groups + target(j, steps[i % CORES], groups)) for i in range(nodes) for j in range(groups)
    ]
    return lax.ppermute(values, ("node", "group"), pairs)


def turns(steps):
    return list(zip(steps[:-2] + steps[-2:][::-1], steps))


def vmem(*shape):
    return pltpu.VMEM(shape, jnp.float32)


def near(*values):
    return [pltpu.with_memory_space_constraint(value, pltpu.VMEM) for value in values]


def far(*values):
    return [pltpu.with_memory_space_constraint(value, pltpu.HBM) for value in values]


def room(*scratch):
    return pltpu.CompilerParams(vmem_limit_bytes=sum(scratch) + (4 << 20))


def place_of():
    node = lax.axis_index("node")
    return node // CORES, lax.rem(node, CORES)


def head_kernel(order, joined, gradient, momentum, worker_error, *rest):
    chips = len(order)
    kept, (sooner, later, error, g_buf, m_buf, w_buf, sems) = rest[:chips], rest[chips:]
    rows, width = momentum.shape
    chip_rows = rows // chips
    shard_rows = chip_rows // CORES
    block_rows = joined * chip_rows
    chip, core = place_of()
    blocks = []
    for at in range(0, chips, joined):
        block = target(chip, order[at], chips) // joined
        part = pl.ds(pl.multiple_of(block * block_rows, block_rows), block_rows)
        pairs = ((gradient.at[0, 0], g_buf), (momentum, m_buf), (worker_error.at[0, 0], w_buf))
        three = [
            pltpu.make_async_copy(src.at[part], dst.at[part], sems.at[at // joined, kind])
            for kind, (src, dst) in enumerate(pairs)
        ]
        for copy in three:
            copy.start()
        blocks.append(three)
    for at, step in enumerate(order):
        if at % joined == 0:
            for copy in blocks[at // joined]:
                copy.wait()
        where = target(chip, step, chips)
        mine = 1 - core if step else core
        for side, half in enumerate((mine, 1 - mine)):
            some = pl.ds(pl.multiple_of(where * chip_rows + half * shard_rows, shard_rows), shard_rows)
            local = 0.9 * m_buf[some, :] + 0.1 * g_buf[some, :].astype(jnp.float32) + w_buf[some, :]
            first = packed_of(local, width)
            if side == 0:
                kept[at][...] = first
            elif at == 0:
                sooner[...] = first
            else:
                later[at - 1] = first
            error[some, :] = local - first


def head(gradient, momentum, worker_error, order):
    rows, width = momentum.shape
    chips = len(order)
    shard = (rows // chips // CORES, width)
    joined = 2 if paired(chips) and chips % 2 == 0 else 1
    return pl.pallas_call(
        functools.partial(head_kernel, order, joined),
        out_shape=[vmem(*shard)] * (chips + 1) + [vmem(chips - 1, *shard), vmem(rows, width)],
        in_specs=[HBM] * 3,
        out_specs=[VMEM] * (chips + 3),
        scratch_shapes=[
            pltpu.VMEM((rows, width), gradient.dtype),
            pltpu.VMEM((rows, width), jnp.float32),
            pltpu.VMEM((rows, width), jnp.float32),
            pltpu.SemaphoreType.DMA((chips // joined, 3)),
        ],
        compiler_params=room(gradient.nbytes, momentum.nbytes, worker_error.nbytes),
    )(*far(gradient, momentum, worker_error))


def server_kernel(nodes, groups, count, *refs):
    parts, (server, worker, piece, second, error_0, error_1) = refs[:count], refs[count:]
    width = server.shape[-1]
    piece_rows = piece.shape[0]
    total = parts[0][...]
    for other in parts[1:]:
        total = total + other[...]
    values = total / nodes + server[...]
    group_q = packed_of(values, width)
    error_0[...] = values - group_q
    values = group_q + worker[...]
    result = packed_of(values, width)
    error_1[...] = values - result
    group = lax.axis_index("group")
    for at in range(groups):
        part = slice(at * piece_rows, (at + 1) * piece_rows)
        second[part, :] = result[part] + jnp.where(group == at, groups * piece[...], jnp.zeros_like(piece))


def serve(parts, server, worker, piece, nodes, groups):
    return pl.pallas_call(
        functools.partial(server_kernel, nodes, groups, len(parts)),
        out_shape=[vmem(*server.shape)] * 3,
        in_specs=[VMEM] * (len(parts) + 3),
        out_specs=[VMEM] * 3,
        compiler_params=room(),
    )(*near(*parts, server, worker, piece))


def store_kernel(count, *refs):
    sems = refs[-1]
    copies = [pltpu.make_async_copy(refs[i], refs[count + i], sems.at[i]) for i in range(count)]
    for copy in copies:
        copy.start()
    for copy in copies:
        copy.wait()


def store(*values):
    count = len(values)
    return pl.pallas_call(
        functools.partial(store_kernel, count),
        out_shape=[pltpu.HBM(value.shape, jnp.float32) for value in values],
        in_specs=[VMEM] * count,
        out_specs=[HBM] * count,
        scratch_shapes=[pltpu.SemaphoreType.DMA((count,))],
        compiler_params=room(),
    )(*near(*values))


def average_kernel(groups, *refs):
    parts, (result, error) = refs[:groups], refs[groups:]
    piece_rows, width = error.shape[1:]
    total = parts[0][...]
    for other in parts[1:]:
        total = total + other[...]
    values = total / groups
    packed = packed_of(values, width)
    result[...] = packed
    for at in range(groups):
        part = slice(at * piece_rows, (at + 1) * piece_rows)
        error[at] = values[part] - packed[part]


def average(parts):
    groups = len(parts)
    rows, width = parts[0].shape
    return pl.pallas_call(
        functools.partial(average_kernel, groups),
        out_shape=[vmem(rows, width), vmem(groups, rows // groups, width)],
        in_specs=[VMEM] * groups,
        out_specs=[VMEM] * 2,
        compiler_params=room(),
    )(*near(*parts))


def update_rows(items, chips, values, variance, params, new_params, new_momentum, p_buf, sems):
    shard_rows = values[0].shape[0]
    chip, core = place_of()
    copies = []
    for at, (step, given) in enumerate(items):
        half = core if crossed_back(step) == given else 1 - core
        start = (source(chip, step, chips) * CORES + half) * shard_rows
        part = pl.ds(pl.multiple_of(start, shard_rows), shard_rows)
        copies.append(pltpu.make_async_copy(values[at], new_momentum.at[part], sems.at[at, 0]))
        copies[-1].start()
        p_buf[at] = params[part, :] - 0.05 * values[at][...] / (jnp.sqrt(variance[part, :]) + 1e-08)
        copies.append(pltpu.make_async_copy(p_buf.at[at], new_params.at[part], sems.at[at, 1]))
        copies[-1].start()
    return copies


def update_kernel(items, chips, *refs):
    count = len(items)
    for copy in update_rows(items, chips, refs[:count], *refs[count : count + 2], *refs[-4:]):
        copy.wait()


def update(values, variance, params, so_far, items, chips):
    count = len(items)
    return pl.pallas_call(
        functools.partial(update_kernel, items, chips),
        out_shape=[pltpu.HBM(params.shape, jnp.float32)] * 2,
        in_specs=[VMEM] * (count + 2) + [HBM] * len(so_far),
        out_specs=[HBM] * 2,
        scratch_shapes=[
            pltpu.VMEM((count, *values[0].shape), jnp.float32),
            pltpu.SemaphoreType.DMA((count, 2)),
        ],
        input_output_aliases={count + 2 + i: i for i in range(len(so_far))},
        compiler_params=room(count * values[0].nbytes),
    )(*near(*values, variance, params), *so_far)


def first_kernel(items, chips, mine, given, variance, params, error, *rest):
    new_params, new_momentum, new_error, p_buf, sems, error_sem = rest
    own = pltpu.make_async_copy(error.at[lax.axis_index("group")], new_error, error_sem)
    own.start()
    outs = (new_params, new_momentum, p_buf, sems)
    for copy in update_rows(items, chips, (mine, given), variance, params, *outs) + [own]:
        copy.wait()


def update_first(mine, given, variance, params, error, chips):
    items = [(0, False), (0, True)]
    return pl.pallas_call(
        functools.partial(first_kernel, items, chips),
        out_shape=[pltpu.HBM(params.shape, jnp.float32)] * 2 + [pltpu.HBM(error.shape[1:], jnp.float32)],
        in_specs=[VMEM] * 5,
        out_specs=[HBM] * 3,
        scratch_shapes=[
            pltpu.VMEM((len(items), *mine.shape), jnp.float32),
            pltpu.SemaphoreType.DMA((len(items), 2)),
            pltpu.SemaphoreType.DMA,
        ],
        compiler_params=room(len(items) * mine.nbytes),
    )(*near(mine, given, variance, params, error))


def body(
    gradient,
    momentum,
    variance,
    params,
    worker_error,
    server_error,
    group_worker_error,
    group_server_error,
):
    nodes = lax.axis_size("node")
    groups = lax.axis_size("group")
    chips = nodes // CORES
    along, back, across = farthest_first(chips), farthest_last(chips), farthest_first(groups)

    *kept, sooner, later, error = head(gradient, momentum, worker_error, along + [0])
    got = [swap_cores(sooner, nodes)]
    got += list(swap_cores(later, nodes))
    parts = [kept[-1], got[-1]]
    for at, step in enumerate(along):
        parts.append(send_chip(kept[at] + got[at], step, nodes, True))

    second, error_0, error_1 = serve(parts, server_error[0], group_worker_error[0], group_server_error, nodes, groups)
    seconds = [second]
    for step, both in zip(across, turns(across)):
        seconds.append(send_group(second, both, nodes, groups))
    new_worker_error, new_server_error, new_group_worker_error = store(error[None, None], error_0[None], error_1[None])

    mine, shard_error = average(seconds)

    arrived = {0: mine}
    for step in back:
        arrived[step] = send_chip(mine, step, nodes, crossed_back(step))
    order = [0] + back
    given = {}
    for step in order:
        given[step] = swap_cores(arrived[step], nodes)
    *outs, new_group_server_error = update_first(mine, given[0], variance, params, shard_error, chips)
    items = [(step, here) for step in order[1:] for here in (False, True)]
    for some in (items[:-1], items[-1:]):
        values = [given[step] if here else arrived[step] for step, here in some]
        outs = update(values, variance, params, outs, some, chips)
    new_params, new_momentum = outs
    return (
        new_params,
        new_momentum,
        new_worker_error,
        new_server_error,
        new_group_worker_error,
        new_group_server_error,
    )


def solution(mesh):
    in_specs = (
        P("node", "group", None, None),
        P(),
        P(),
        P(),
        P("node", "group", None, None),
        P("group", "node", None),
        P("group", "node", None),
        P(("node", "group"), None),
    )
    out_specs = (
        P(),
        P(),
        P("node", "group", None, None),
        P("group", "node", None),
        P("group", "node", None),
        P(("node", "group"), None),
    )
    return jax.shard_map(body, mesh=mesh, in_specs=in_specs, out_specs=out_specs, check_vma=False)
```

profile of v0, /device:TPU:0, one launch (start us, length us, event | category | flops | bytes accessed | tf_op | source)
XLA Modules:
  0.0 34.0 jit_solution(198456296620507038)
XLA Ops:
  0.6 1.5 %shard_map.127 = (f32[16,1024]{1,0:T(8,128)S(1)}, f32[16,1024]{1,0:T(8,128)S(1)}, f32[16,1024]{1,0:T(8,128)S(1)}, f32[16,1024]{1,0:T(8,128)S(1)}, f32[16,1024]{1...) custom-call(bf16[1,1,128,1024]{3,2,1,0:T(8,128)(2,1)} %gradient.1, f32[128,1024]{1,0:T(8,128)} %momentum.1, ...), custom_call_target="tpu_custom_call" | custom-call | tf_op jit(solution)/shard_map/pallas_call | solution.py:137
  2.2 0.6 %collective-permute-start = (f32[3,16,1024]{2,1,0:T(8,128)S(1)}, f32[3,16,1024]{2,1,0:T(8,128)S(1)}, u32[]{:S(2)}, u32[]{:S(2)}) collective-permute-start(f32[3,16,1024]{2,1,0:T(8,128)S(1)} %get-tuple-element.29), channel_id=1, source_target_pairs={{0,4},{4,0},{8,12},{12,8},{16,20},{20,16},{24,28},{28,24},{1,5},{5... | collective-permute-start | bytes 589832 | tf_op jit(solution)/shard_map/ppermute | solution.py:48
  2.7 0.1 collective-permute-start.1
  2.8 1.2 %collective-permute-done.1 = f32[16,1024]{1,0:T(8,128)S(1)} collective-permute-done((f32[16,1024]{1,0:T(8,128)S(1)}, f32[16,1024]{1,0:T(8,128)S(1)}, u32[]{:S(2)}, u32[]{:S(2)}) %collective-permute-start.1) | collective-permute-done | bytes 65568 | tf_op jit(solution)/shard_map/ppermute | solution.py:48
  4.0 4.8 %collective-permute-start.2 = (f32[16,1024]{1,0:T(8,128)S(1)}, f32[16,1024]{1,0:T(8,128)S(1)}, u32[]{:S(2)}, u32[]{:S(2)}) collective-permute-start(f32[16,1024]{1,0:T(8,128)S(1)} %add.9), channel_id=1, source_target_pairs={{0,28},{4,24},{8,20},{12,16},{16,12},{20,8},{24,4},{28,0},{1,29},{... | collective-permute-start | bytes 196616 | tf_op jit(solution)/shard_map/ppermute | solution.py:58
  8.8 0.0 collective-permute-done
  8.8 0.0 copy-start.4
  8.8 0.1 collective-permute-start.3
  8.9 0.0 copy-start.2
  8.9 0.0 copy-start.3
  8.9 0.5 %collective-permute-start.4 = (f32[16,1024]{1,0:T(8,128)S(1)}, f32[16,1024]{1,0:T(8,128)S(1)}, u32[]{:S(2)}, u32[]{:S(2)}) collective-permute-start(f32[16,1024]{1,0:T(8,128)S(1)} %get-tuple-element.50), channel_id=1, source_target_pairs={{0,12},{4,8},{8,4},{12,0},{16,28},{20,24},{24,20},{28,16},{1,13},{... | collective-permute-start | bytes 196616 | tf_op jit(solution)/shard_map/ppermute | solution.py:58
  9.3 1.9 %collective-permute-done.2.refs_2_ = f32[16,1024]{1,0:T(8,128)S(1)} collective-permute-done((f32[16,1024]{1,0:T(8,128)S(1)}, f32[16,1024]{1,0:T(8,128)S(1)}, u32[]{:S(2)}, u32[]{:S(2)}) %collective-permute-start.2) | collective-permute-done | bytes 65568 | tf_op jit(solution)/shard_map/ppermute | solution.py:58
  11.3 3.2 %collective-permute-done.3.refs_3_ = f32[16,1024]{1,0:T(8,128)S(1)} collective-permute-done((f32[16,1024]{1,0:T(8,128)S(1)}, f32[16,1024]{1,0:T(8,128)S(1)}, u32[]{:S(2)}, u32[]{:S(2)}) %collective-permute-start.3) | collective-permute-done | bytes 65568 | tf_op jit(solution)/shard_map/ppermute | solution.py:58
  14.5 0.0 collective-permute-done.4.refs_4_
  14.5 0.0 copy-done.4
  14.5 0.0 copy-done.2
  14.5 0.0 copy-done.3
  14.6 0.0 copy-start.1
  14.6 0.2 shard_map.128
  14.8 0.0 copy-start
  14.8 2.5 %collective-permute-start.5 = (f32[16,1024]{1,0:T(8,128)S(1)}, f32[16,1024]{1,0:T(8,128)S(1)}, u32[]{:S(2)}, u32[]{:S(2)}) collective-permute-start(f32[16,1024]{1,0:T(8,128)S(1)} %get-tuple-element.34.refs_0_), channel_id=1, source_target_pairs={{0,3},{1,2},{2,1},{3,0},{4,7},{5,6},{6,5},{7,4},{8,11},{9,10},{10,... | collective-permute-start | bytes 196616 | tf_op jit(solution)/shard_map/ppermute | solution.py:65
  17.3 0.5 %collective-permute-start.6 = (f32[16,1024]{1,0:T(8,128)S(1)}, f32[16,1024]{1,0:T(8,128)S(1)}, u32[]{:S(2)}, u32[]{:S(2)}) collective-permute-start(f32[16,1024]{1,0:T(8,128)S(1)} %get-tuple-element.34.refs_0_), channel_id=1, source_target_pairs={{0,1},{1,0},{2,3},{3,2},{4,6},{5,7},{6,4},{7,5},{8,9},{9,8},{10,11... | collective-permute-start | bytes 196616 | tf_op jit(solution)/shard_map/ppermute | solution.py:65
  17.8 0.5 %collective-permute-start.7 = (f32[16,1024]{1,0:T(8,128)S(1)}, f32[16,1024]{1,0:T(8,128)S(1)}, u32[]{:S(2)}, u32[]{:S(2)}) collective-permute-start(f32[16,1024]{1,0:T(8,128)S(1)} %get-tuple-element.34.refs_0_), channel_id=1, source_target_pairs={{0,2},{1,3},{2,0},{3,1},{4,5},{5,4},{6,7},{7,6},{8,10},{9,11},{10,... | collective-permute-start | bytes 196616 | tf_op jit(solution)/shard_map/ppermute | solution.py:65
  18.3 1.7 %collective-permute-done.5.refs_1_ = f32[16,1024]{1,0:T(8,128)S(1)} collective-permute-done((f32[16,1024]{1,0:T(8,128)S(1)}, f32[16,1024]{1,0:T(8,128)S(1)}, u32[]{:S(2)}, u32[]{:S(2)}) %collective-permute-start.5) | collective-permute-done | bytes 65568 | tf_op jit(solution)/shard_map/ppermute | solution.py:65
  20.0 1.5 %collective-permute-done.6.refs_2_ = f32[16,1024]{1,0:T(8,128)S(1)} collective-permute-done((f32[16,1024]{1,0:T(8,128)S(1)}, f32[16,1024]{1,0:T(8,128)S(1)}, u32[]{:S(2)}, u32[]{:S(2)}) %collective-permute-start.6) | collective-permute-done | bytes 65568 | tf_op jit(solution)/shard_map/ppermute | solution.py:65
  21.6 0.5 %collective-permute-done.7.refs_3_ = f32[16,1024]{1,0:T(8,128)S(1)} collective-permute-done((f32[16,1024]{1,0:T(8,128)S(1)}, f32[16,1024]{1,0:T(8,128)S(1)}, u32[]{:S(2)}, u32[]{:S(2)}) %collective-permute-start.7) | collective-permute-done | bytes 65568 | tf_op jit(solution)/shard_map/ppermute | solution.py:65
  22.1 0.1 shard_map.129
  22.2 0.1 collective-permute-start.10
  22.3 1.3 %collective-permute-start.12 = (f32[16,1024]{1,0:T(8,128)S(1)}, f32[16,1024]{1,0:T(8,128)S(1)}, u32[]{:S(2)}, u32[]{:S(2)}) collective-permute-start(f32[16,1024]{1,0:T(8,128)S(1)} %get-tuple-element.35.mine), channel_id=1, source_target_pairs={{0,8},{4,12},{8,0},{12,4},{16,24},{20,28},{24,16},{28,20},{1,9},{5... | collective-permute-start | bytes 196616 | tf_op jit(solution)/shard_map/ppermute | solution.py:58
  23.6 1.5 %collective-permute-start.8 = (f32[16,1024]{1,0:T(8,128)S(1)}, f32[16,1024]{1,0:T(8,128)S(1)}, u32[]{:S(2)}, u32[]{:S(2)}) collective-permute-start(f32[16,1024]{1,0:T(8,128)S(1)} %get-tuple-element.35.mine), channel_id=1, source_target_pairs={{0,24},{4,28},{8,16},{12,20},{16,8},{20,12},{24,0},{28,4},{1,25},{... | collective-permute-start | bytes 196616 | tf_op jit(solution)/shard_map/ppermute | solution.py:58
  25.1 1.1 %collective-permute-start.14 = (f32[16,1024]{1,0:T(8,128)S(1)}, f32[16,1024]{1,0:T(8,128)S(1)}, u32[]{:S(2)}, u32[]{:S(2)}) collective-permute-start(f32[16,1024]{1,0:T(8,128)S(1)} %get-tuple-element.35.mine), channel_id=1, source_target_pairs={{0,4},{4,0},{8,12},{12,8},{16,20},{20,16},{24,28},{28,24},{1,5},{5... | collective-permute-start | bytes 196616 | tf_op jit(solution)/shard_map/ppermute | solution.py:48
  26.2 2.4 %collective-permute-done.10.refs_0_ = f32[16,1024]{1,0:T(8,128)S(1)} collective-permute-done((f32[16,1024]{1,0:T(8,128)S(1)}, f32[16,1024]{1,0:T(8,128)S(1)}, u32[]{:S(2)}, u32[]{:S(2)}) %collective-permute-start.10) | collective-permute-done | bytes 65568 | tf_op jit(solution)/shard_map/ppermute | solution.py:58
  28.6 0.0 collective-permute-start.11
  28.6 0.0 collective-permute-done.12.refs_2_
  28.6 0.5 %collective-permute-start.13 = (f32[16,1024]{1,0:T(8,128)S(1)}, f32[16,1024]{1,0:T(8,128)S(1)}, u32[]{:S(2)}, u32[]{:S(2)}) collective-permute-start(f32[16,1024]{1,0:T(8,128)S(1)} %collective-permute-done.12.refs_2_), channel_id=1, source_target_pairs={{0,4},{4,0},{8,12},{12,8},{16,20},{20,16},{24,28},{28,24},{1,5},{5... | collective-permute-start | bytes 196616 | tf_op jit(solution)/shard_map/ppermute | solution.py:48
  29.1 1.3 %collective-permute-done.8.refs_4_ = f32[16,1024]{1,0:T(8,128)S(1)} collective-permute-done((f32[16,1024]{1,0:T(8,128)S(1)}, f32[16,1024]{1,0:T(8,128)S(1)}, u32[]{:S(2)}, u32[]{:S(2)}) %collective-permute-start.8) | collective-permute-done | bytes 65568 | tf_op jit(solution)/shard_map/ppermute | solution.py:58
  30.4 0.2 collective-permute-start.9
  30.6 0.8 %shard_map.133 = (f32[1,1,128,1024]{3,2,1,0:T(8,128)}, f32[1,16,1024]{2,1,0:T(8,128)}, f32[1,16,1024]{2,1,0:T(8,128)}) custom-call(f32[1,1,128,1024]{3,2,1,0:T(8,128)S(1)} %bitcast.15, f32[1,16,1024]{2,1,0:T(8,128)S(1)} %bitcast.16, f32[1,16,1024]{2,1,0:T(8,128)S(1)} %bitcast.17), custom_call_target="tpu_custom_call" | custom-call | tf_op jit(solution)/shard_map/pallas_call | solution.py:192
  31.5 0.0 collective-permute-done.14.given
  31.5 0.0 copy-done.1
  31.5 0.0 copy-done
  31.5 0.8 %shard_map.130 = (f32[128,1024]{1,0:T(8,128)}, f32[128,1024]{1,0:T(8,128)}, f32[4,1024]{1,0:T(4,128)}) custom-call(f32[16,1024]{1,0:T(8,128)S(1)} %get-tuple-element.35.mine, f32[16,1024]{1,0:T(8,128)S(1)} %collective-permute-done.14.given, f32[128,1024]{1,0:T(8,128)S(1)} %copy-done, f32[128,1024]{1,0:T(8,128)S(1)} %copy-done.1, ...), custom_call_target="tpu_custom_call" | custom-call | tf_op jit(solution)/shard_map/pallas_call | solution.py:277
  32.3 0.0 collective-permute-done.11.refs_1_
  32.3 0.0 collective-permute-done.13.refs_3_
  32.3 1.0 %shard_map.131 = (f32[128,1024]{1,0:T(8,128)}, f32[128,1024]{1,0:T(8,128)}) custom-call(f32[16,1024]{1,0:T(8,128)S(1)} %collective-permute-done.10.refs_0_, f32[16,1024]{1,0:T(8,128)S(1)} %collective-permute-done.11.refs_1_, f32[16,1024]{1,0:T(8,128)S(1)} %collective-permute-done.12.refs_2_, ...), custom_call_target="tpu_custom_call", output_to_operand_aliasing={{0}: (7, {}), {1}: (8, {})} | custom-call | tf_op jit(solution)/shard_map/pallas_call | solution.py:252
  33.3 0.0 collective-permute-done.9.refs_0_
  33.3 0.7 %shard_map.132 = (f32[128,1024]{1,0:T(8,128)}, f32[128,1024]{1,0:T(8,128)}) custom-call(f32[16,1024]{1,0:T(8,128)S(1)} %collective-permute-done.9.refs_0_, f32[128,1024]{1,0:T(8,128)S(1)} %copy-done, f32[128,1024]{1,0:T(8,128)S(1)} %copy-done.1, f32[128,1024]{1,0:T(8,128)} %get-tuple-element.39.refs_3_, ...), custom_call_target="tpu_custom_call", output_to_operand_aliasing={{0}: (3, {}), {1}: (4, {})} | custom-call | tf_op jit(solution)/shard_map/pallas_call | solution.py:252
  (3 shorter events, 0.0 us)
Async XLA Ops:
  2.2 6.6 %collective-permute-start = (f32[3,16,1024]{2,1,0:T(8,128)S(1)}, f32[3,16,1024]{2,1,0:T(8,128)S(1)}, u32[]{:S(2)}, u32[]{:S(2)}) collective-permute-start(f32[3,16,1024]{2,1,0:T(8,128)S(1)} %get-tuple-element.29), channel_id=1, source_target_pairs={{0,4},{4,0},{8,12},{12,8},{16,20},{20,16},{24,28},{28,24},{1,5},{5... | collective-permute-start | bytes 589832 | tf_op jit(solution)/shard_map/ppermute | solution.py:48
  2.7 1.3 %collective-permute-start.1 = (f32[16,1024]{1,0:T(8,128)S(1)}, f32[16,1024]{1,0:T(8,128)S(1)}, u32[]{:S(2)}, u32[]{:S(2)}) collective-permute-start(f32[16,1024]{1,0:T(8,128)S(1)} %get-tuple-element.31), channel_id=1, source_target_pairs={{0,4},{4,0},{8,12},{12,8},{16,20},{20,16},{24,28},{28,24},{1,5},{5... | collective-permute-start | bytes 196616 | tf_op jit(solution)/shard_map/ppermute | solution.py:48
  4.0 7.3 %collective-permute-start.2 = (f32[16,1024]{1,0:T(8,128)S(1)}, f32[16,1024]{1,0:T(8,128)S(1)}, u32[]{:S(2)}, u32[]{:S(2)}) collective-permute-start(f32[16,1024]{1,0:T(8,128)S(1)} %add.9), channel_id=1, source_target_pairs={{0,28},{4,24},{8,20},{12,16},{16,12},{20,8},{24,4},{28,0},{1,29},{... | collective-permute-start | bytes 196616 | tf_op jit(solution)/shard_map/ppermute | solution.py:58
  8.8 5.8 %copy-start.4 = (f32[4,1024]{1,0:T(4,128)S(1)}, f32[4,1024]{1,0:T(4,128)}, u32[]{:S(2)}) copy-start(f32[4,1024]{1,0:T(4,128)} %refs_7_.1) | copy-start | bytes 49156
  8.8 5.7 %collective-permute-start.3 = (f32[16,1024]{1,0:T(8,128)S(1)}, f32[16,1024]{1,0:T(8,128)S(1)}, u32[]{:S(2)}, u32[]{:S(2)}) collective-permute-start(f32[16,1024]{1,0:T(8,128)S(1)} %get-tuple-element.51), channel_id=1, source_target_pairs={{0,20},{4,16},{8,28},{12,24},{16,4},{20,0},{24,12},{28,8},{1,21},{... | collective-permute-start | bytes 196616 | tf_op jit(solution)/shard_map/ppermute | solution.py:58
  8.9 5.7 %copy-start.2 = (f32[1,16,1024]{2,1,0:T(8,128)S(1)}, f32[1,16,1024]{2,1,0:T(8,128)}, u32[]{:S(2)}) copy-start(f32[1,16,1024]{2,1,0:T(8,128)} %param.13) | copy-start | bytes 196612
  8.9 5.7 %copy-start.3 = (f32[1,16,1024]{2,1,0:T(8,128)S(1)}, f32[1,16,1024]{2,1,0:T(8,128)}, u32[]{:S(2)}) copy-start(f32[1,16,1024]{2,1,0:T(8,128)} %param.14) | copy-start | bytes 196612
  8.9 5.6 %collective-permute-start.4 = (f32[16,1024]{1,0:T(8,128)S(1)}, f32[16,1024]{1,0:T(8,128)S(1)}, u32[]{:S(2)}, u32[]{:S(2)}) collective-permute-start(f32[16,1024]{1,0:T(8,128)S(1)} %get-tuple-element.50), channel_id=1, source_target_pairs={{0,12},{4,8},{8,4},{12,0},{16,28},{20,24},{24,20},{28,16},{1,13},{... | collective-permute-start | bytes 196616 | tf_op jit(solution)/shard_map/ppermute | solution.py:58
  14.6 17.0 %copy-start.1 = (f32[128,1024]{1,0:T(8,128)S(1)}, f32[128,1024]{1,0:T(8,128)}, u32[]{:S(2)}) copy-start(f32[128,1024]{1,0:T(8,128)} %refs_2_.1) | copy-start | bytes 1572868
  14.8 16.7 %copy-start = (f32[128,1024]{1,0:T(8,128)S(1)}, f32[128,1024]{1,0:T(8,128)}, u32[]{:S(2)}) copy-start(f32[128,1024]{1,0:T(8,128)} %refs_1_.1) | copy-start | bytes 1572868
  14.8 5.2 %collective-permute-start.5 = (f32[16,1024]{1,0:T(8,128)S(1)}, f32[16,1024]{1,0:T(8,128)S(1)}, u32[]{:S(2)}, u32[]{:S(2)}) collective-permute-start(f32[16,1024]{1,0:T(8,128)S(1)} %get-tuple-element.34.refs_0_), channel_id=1, source_target_pairs={{0,3},{1,2},{2,1},{3,0},{4,7},{5,6},{6,5},{7,4},{8,11},{9,10},{10,... | collective-permute-start | bytes 196616 | tf_op jit(solution)/shard_map/ppermute | solution.py:65
  17.3 4.3 %collective-permute-start.6 = (f32[16,1024]{1,0:T(8,128)S(1)}, f32[16,1024]{1,0:T(8,128)S(1)}, u32[]{:S(2)}, u32[]{:S(2)}) collective-permute-start(f32[16,1024]{1,0:T(8,128)S(1)} %get-tuple-element.34.refs_0_), channel_id=1, source_target_pairs={{0,1},{1,0},{2,3},{3,2},{4,6},{5,7},{6,4},{7,5},{8,9},{9,8},{10,11... | collective-permute-start | bytes 196616 | tf_op jit(solution)/shard_map/ppermute | solution.py:65
  17.8 4.3 %collective-permute-start.7 = (f32[16,1024]{1,0:T(8,128)S(1)}, f32[16,1024]{1,0:T(8,128)S(1)}, u32[]{:S(2)}, u32[]{:S(2)}) collective-permute-start(f32[16,1024]{1,0:T(8,128)S(1)} %get-tuple-element.34.refs_0_), channel_id=1, source_target_pairs={{0,2},{1,3},{2,0},{3,1},{4,5},{5,4},{6,7},{7,6},{8,10},{9,11},{10,... | collective-permute-start | bytes 196616 | tf_op jit(solution)/shard_map/ppermute | solution.py:65
  22.2 6.4 %collective-permute-start.10 = (f32[16,1024]{1,0:T(8,128)S(1)}, f32[16,1024]{1,0:T(8,128)S(1)}, u32[]{:S(2)}, u32[]{:S(2)}) collective-permute-start(f32[16,1024]{1,0:T(8,128)S(1)} %get-tuple-element.35.mine), channel_id=1, source_target_pairs={{0,20},{4,16},{8,28},{12,24},{16,4},{20,0},{24,12},{28,8},{1,21},{... | collective-permute-start | bytes 196616 | tf_op jit(solution)/shard_map/ppermute | solution.py:58
  22.3 6.3 %collective-permute-start.12 = (f32[16,1024]{1,0:T(8,128)S(1)}, f32[16,1024]{1,0:T(8,128)S(1)}, u32[]{:S(2)}, u32[]{:S(2)}) collective-permute-start(f32[16,1024]{1,0:T(8,128)S(1)} %get-tuple-element.35.mine), channel_id=1, source_target_pairs={{0,8},{4,12},{8,0},{12,4},{16,24},{20,28},{24,16},{28,20},{1,9},{5... | collective-permute-start | bytes 196616 | tf_op jit(solution)/shard_map/ppermute | solution.py:58
  23.6 6.8 %collective-permute-start.8 = (f32[16,1024]{1,0:T(8,128)S(1)}, f32[16,1024]{1,0:T(8,128)S(1)}, u32[]{:S(2)}, u32[]{:S(2)}) collective-permute-start(f32[16,1024]{1,0:T(8,128)S(1)} %get-tuple-element.35.mine), channel_id=1, source_target_pairs={{0,24},{4,28},{8,16},{12,20},{16,8},{20,12},{24,0},{28,4},{1,25},{... | collective-permute-start | bytes 196616 | tf_op jit(solution)/shard_map/ppermute | solution.py:58
  25.1 6.4 %collective-permute-start.14 = (f32[16,1024]{1,0:T(8,128)S(1)}, f32[16,1024]{1,0:T(8,128)S(1)}, u32[]{:S(2)}, u32[]{:S(2)}) collective-permute-start(f32[16,1024]{1,0:T(8,128)S(1)} %get-tuple-element.35.mine), channel_id=1, source_target_pairs={{0,4},{4,0},{8,12},{12,8},{16,20},{20,16},{24,28},{28,24},{1,5},{5... | collective-permute-start | bytes 196616 | tf_op jit(solution)/shard_map/ppermute | solution.py:48
  28.6 3.7 %collective-permute-start.11 = (f32[16,1024]{1,0:T(8,128)S(1)}, f32[16,1024]{1,0:T(8,128)S(1)}, u32[]{:S(2)}, u32[]{:S(2)}) collective-permute-start(f32[16,1024]{1,0:T(8,128)S(1)} %collective-permute-done.10.refs_0_), channel_id=1, source_target_pairs={{0,4},{4,0},{8,12},{12,8},{16,20},{20,16},{24,28},{28,24},{1,5},{5... | collective-permute-start | bytes 196616 | tf_op jit(solution)/shard_map/ppermute | solution.py:48
  28.6 3.7 %collective-permute-start.13 = (f32[16,1024]{1,0:T(8,128)S(1)}, f32[16,1024]{1,0:T(8,128)S(1)}, u32[]{:S(2)}, u32[]{:S(2)}) collective-permute-start(f32[16,1024]{1,0:T(8,128)S(1)} %collective-permute-done.12.refs_2_), channel_id=1, source_target_pairs={{0,4},{4,0},{8,12},{12,8},{16,20},{20,16},{24,28},{28,24},{1,5},{5... | collective-permute-start | bytes 196616 | tf_op jit(solution)/shard_map/ppermute | solution.py:48
  30.4 2.9 %collective-permute-start.9 = (f32[16,1024]{1,0:T(8,128)S(1)}, f32[16,1024]{1,0:T(8,128)S(1)}, u32[]{:S(2)}, u32[]{:S(2)}) collective-permute-start(f32[16,1024]{1,0:T(8,128)S(1)} %collective-permute-done.8.refs_4_), channel_id=1, source_target_pairs={{0,4},{4,0},{8,12},{12,8},{16,20},{20,16},{24,28},{28,24},{1,5},{5... | collective-permute-start | bytes 196616 | tf_op jit(solution)/shard_map/ppermute | solution.py:48
where the time goes:
time: 34.2 us; the launch traced here: 34 us
  starting transfers between devices  14.2 us (42%)
  waiting for transfers between devices  13.8 us (40%)
  Pallas kernels  5.12 us (15%)
  between operations  0.8 us (2%)
    ppermute x6, waiting for transfers between devices, send_chip(): return lax.ppermute(values, 'node', pairs)  8.87 us
    ppermute x6, starting transfers between devices, send_chip(): return lax.ppermute(values, 'node', pairs)  8.14 us
    ppermute x3, waiting for transfers between devices, send_group(): return lax.ppermute(values, ('node', 'group'), pairs)  3.76 us
    ppermute x3, starting transfers between devices, send_group(): return lax.ppermute(values, ('node', 'group'), pairs)  3.55 us
    ppermute x6, starting transfers between devices, swap_cores(): return lax.ppermute(values, 'node', [(i, i ^ 1) for i in range(nodes)])  2.51 us
    pallas_call x2, Pallas kernels, update(): pl.pallas_call(functools.partial(update_kernel, items, chips), out_shape=...  1.66 us
    pallas_call x1, Pallas kernels, head(): pl.pallas_call(functools.partial(head_kernel, order, joined), out_shape=[...  1.53 us
    ppermute x6, waiting for transfers between devices, swap_cores(): return lax.ppermute(values, 'node', [(i, i ^ 1) for i in range(nodes)])  1.19 us
  transfers between devices with their start and end apart: 15, of which 8 were waited for; matrix products, arithmetic and copies ran while one was open for 0% of the time, Pallas kernels for 8%

commit v1 on v0

--- a/solution.py
+++ b/solution.py
@@ -58,15 +58,8 @@
     return lax.ppermute(values, "node", pairs)
 
 
-def send_group(values, steps, nodes, groups):
-    pairs = [
-        (i * groups + j, i * groups + target(j, steps[i % CORES], groups)) for i in range(nodes) for j in range(groups)
-    ]
-    return lax.ppermute(values, ("node", "group"), pairs)
-
-
-def turns(steps):
-    return list(zip(steps[:-2] + steps[-2:][::-1], steps))
+def send_group(values, step, groups):
+    return lax.ppermute(values, "group", [(i, target(i, step, groups)) for i in range(groups)])
 
 
 def vmem(*shape):
@@ -310,18 +303,22 @@
     for at, step in enumerate(along):
         parts.append(send_chip(kept[at] + got[at], step, nodes, True))
 
-    second, error_0, error_1 = serve(parts, server_error[0], group_worker_error[0], group_server_error, nodes, groups)
+    second, error_0, error_1 = serve(
+        parts, server_error[0], group_worker_error[0], group_server_error, nodes, groups
+    )
     seconds = [second]
-    for step, both in zip(across, turns(across)):
-        seconds.append(send_group(second, both, nodes, groups))
-    new_worker_error, new_server_error, new_group_worker_error = store(error[None, None], error_0[None], error_1[None])
+    for step in across:
+        seconds.append(send_group(second, step, groups))
+    new_worker_error, new_server_error, new_group_worker_error = store(
+        error[None, None], error_0[None], error_1[None]
+    )
 
     mine, shard_error = average(seconds)
 
     arrived = {0: mine}
     for step in back:
         arrived[step] = send_chip(mine, step, nodes, crossed_back(step))
-    order = [0] + back
+    order = [0] + sorted(back)
     given = {}
     for step in order:
         given[step] = swap_cores(arrived[step], nodes)

time: 34.2 us -> 35.5 us (1.038)
  waiting for transfers between devices: 13.8 us -> 15.1 us
    ppermute x6, waiting for transfers between devices: 8.87 us -> 10.2 us  [send_chip(): return lax.ppermute(values, 'node', pairs)]
  transfers between devices with their start and end apart: 15 -> 15, of which waited for: 8 -> 7; matrix products, arithmetic and copies ran while one was open for 0% -> 0% of each run, Pallas kernels for 8% -> 7%
where the time goes in v1:
time: 35.5 us; the launch traced here: 35.3 us
  waiting for transfers between devices  15.1 us (43%)
  starting transfers between devices  14.3 us (40%)
  Pallas kernels  5.12 us (14%)
  between operations  0.79 us (2%)
    ppermute x6, waiting for transfers between devices, send_chip(): return lax.ppermute(values, 'node', pairs)  10.2 us
    ppermute x6, starting transfers between devices, send_chip(): return lax.ppermute(values, 'node', pairs)  8.15 us
    ppermute x3, waiting for transfers between devices, send_group(): lax.ppermute(values, 'group', [(i, target(i, step, groups)) for i in rang...  3.73 us
    ppermute x3, starting transfers between devices, send_group(): lax.ppermute(values, 'group', [(i, target(i, step, groups)) for i in rang...  3.55 us
    ppermute x6, starting transfers between devices, swap_cores(): return lax.ppermute(values, 'node', [(i, i ^ 1) for i in range(nodes)])  2.57 us
    pallas_call x2, Pallas kernels, update(): pl.pallas_call(functools.partial(update_kernel, items, chips), out_shape=...  1.66 us
    pallas_call x1, Pallas kernels, head(): pl.pallas_call(functools.partial(head_kernel, order, joined), out_shape=[...  1.53 us
    ppermute x6, waiting for transfers between devices, swap_cores(): return lax.ppermute(values, 'node', [(i, i ^ 1) for i in range(nodes)])  1.19 us
  transfers between devices with their start and end apart: 15, of which 7 were waited for; matrix products, arithmetic and copies ran while one was open for 0% of the time, Pallas kernels for 7%

profile of v1, /device:TPU:0, one launch (start us, length us, event | category | flops | bytes accessed | tf_op | source)
XLA Modules:
  0.0 35.3 jit_solution(11833232696489897923)
XLA Ops:
  0.6 1.5 %shard_map.127 = (f32[16,1024]{1,0:T(8,128)S(1)}, f32[16,1024]{1,0:T(8,128)S(1)}, f32[16,1024]{1,0:T(8,128)S(1)}, f32[16,1024]{1,0:T(8,128)S(1)}, f32[16,1024]{1...) custom-call(bf16[1,1,128,1024]{3,2,1,0:T(8,128)(2,1)} %gradient.1, f32[128,1024]{1,0:T(8,128)} %momentum.1, ...), custom_call_target="tpu_custom_call" | custom-call | tf_op jit(solution)/shard_map/pallas_call | solution.py:130
  2.2 0.6 %collective-permute-start = (f32[3,16,1024]{2,1,0:T(8,128)S(1)}, f32[3,16,1024]{2,1,0:T(8,128)S(1)}, u32[]{:S(2)}, u32[]{:S(2)}) collective-permute-start(f32[3,16,1024]{2,1,0:T(8,128)S(1)} %get-tuple-element.29), channel_id=1, source_target_pairs={{0,4},{4,0},{8,12},{12,8},{16,20},{20,16},{24,28},{28,24},{1,5},{5... | collective-permute-start | bytes 589832 | tf_op jit(solution)/shard_map/ppermute | solution.py:48
  2.7 0.1 collective-permute-start.1
  2.8 1.2 %collective-permute-done.1 = f32[16,1024]{1,0:T(8,128)S(1)} collective-permute-done((f32[16,1024]{1,0:T(8,128)S(1)}, f32[16,1024]{1,0:T(8,128)S(1)}, u32[]{:S(2)}, u32[]{:S(2)}) %collective-permute-start.1) | collective-permute-done | bytes 65568 | tf_op jit(solution)/shard_map/ppermute | solution.py:48
  4.0 4.8 %collective-permute-start.2 = (f32[16,1024]{1,0:T(8,128)S(1)}, f32[16,1024]{1,0:T(8,128)S(1)}, u32[]{:S(2)}, u32[]{:S(2)}) collective-permute-start(f32[16,1024]{1,0:T(8,128)S(1)} %add.9), channel_id=1, source_target_pairs={{0,28},{4,24},{8,20},{12,16},{16,12},{20,8},{24,4},{28,0},{1,29},{... | collective-permute-start | bytes 196616 | tf_op jit(solution)/shard_map/ppermute | solution.py:58
  8.8 0.0 collective-permute-done
  8.8 0.0 copy-start.4
  8.8 0.1 collective-permute-start.3
  8.9 0.0 copy-start.2
  8.9 0.0 copy-start.3
  8.9 0.5 %collective-permute-start.4 = (f32[16,1024]{1,0:T(8,128)S(1)}, f32[16,1024]{1,0:T(8,128)S(1)}, u32[]{:S(2)}, u32[]{:S(2)}) collective-permute-start(f32[16,1024]{1,0:T(8,128)S(1)} %get-tuple-element.50), channel_id=1, source_target_pairs={{0,12},{4,8},{8,4},{12,0},{16,28},{20,24},{24,20},{28,16},{1,13},{... | collective-permute-start | bytes 196616 | tf_op jit(solution)/shard_map/ppermute | solution.py:58
  9.3 1.9 %collective-permute-done.2.refs_2_ = f32[16,1024]{1,0:T(8,128)S(1)} collective-permute-done((f32[16,1024]{1,0:T(8,128)S(1)}, f32[16,1024]{1,0:T(8,128)S(1)}, u32[]{:S(2)}, u32[]{:S(2)}) %collective-permute-start.2) | collective-permute-done | bytes 65568 | tf_op jit(solution)/shard_map/ppermute | solution.py:58
  11.3 3.2 %collective-permute-done.3.refs_3_ = f32[16,1024]{1,0:T(8,128)S(1)} collective-permute-done((f32[16,1024]{1,0:T(8,128)S(1)}, f32[16,1024]{1,0:T(8,128)S(1)}, u32[]{:S(2)}, u32[]{:S(2)}) %collective-permute-start.3) | collective-permute-done | bytes 65568 | tf_op jit(solution)/shard_map/ppermute | solution.py:58
  14.5 0.0 collective-permute-done.4.refs_4_
  14.5 0.0 copy-done.4
  14.5 0.0 copy-done.2
  14.5 0.0 copy-done.3
  14.6 0.0 copy-start.1
  14.6 0.2 shard_map.128
  14.8 0.0 copy-start
  14.8 2.5 %collective-permute-start.5 = (f32[16,1024]{1,0:T(8,128)S(1)}, f32[16,1024]{1,0:T(8,128)S(1)}, u32[]{:S(2)}, u32[]{:S(2)}) collective-permute-start(f32[16,1024]{1,0:T(8,128)S(1)} %get-tuple-element.34.refs_0_), channel_id=1, source_target_pairs={{0,3},{1,2},{2,1},{3,0},{4,7},{5,6},{6,5},{7,4},{8,11},{9,10},{10,... | collective-permute-start | bytes 196616 | tf_op jit(solution)/shard_map/ppermute | solution.py:62
  17.3 0.5 %collective-permute-start.6 = (f32[16,1024]{1,0:T(8,128)S(1)}, f32[16,1024]{1,0:T(8,128)S(1)}, u32[]{:S(2)}, u32[]{:S(2)}) collective-permute-start(f32[16,1024]{1,0:T(8,128)S(1)} %get-tuple-element.34.refs_0_), channel_id=1, source_target_pairs={{0,2},{1,3},{2,0},{3,1},{4,6},{5,7},{6,4},{7,5},{8,10},{9,11},{10,... | collective-permute-start | bytes 196616 | tf_op jit(solution)/shard_map/ppermute | solution.py:62
  17.8 0.5 %collective-permute-start.7 = (f32[16,1024]{1,0:T(8,128)S(1)}, f32[16,1024]{1,0:T(8,128)S(1)}, u32[]{:S(2)}, u32[]{:S(2)}) collective-permute-start(f32[16,1024]{1,0:T(8,128)S(1)} %get-tuple-element.34.refs_0_), channel_id=1, source_target_pairs={{0,1},{1,0},{2,3},{3,2},{4,5},{5,4},{6,7},{7,6},{8,9},{9,8},{10,11... | collective-permute-start | bytes 196616 | tf_op jit(solution)/shard_map/ppermute | solution.py:62
  18.3 1.7 %collective-permute-done.5.refs_1_ = f32[16,1024]{1,0:T(8,128)S(1)} collective-permute-done((f32[16,1024]{1,0:T(8,128)S(1)}, f32[16,1024]{1,0:T(8,128)S(1)}, u32[]{:S(2)}, u32[]{:S(2)}) %collective-permute-start.5) | collective-permute-done | bytes 65568 | tf_op jit(solution)/shard_map/ppermute | solution.py:62
  20.0 1.5 %collective-permute-done.6.refs_2_ = f32[16,1024]{1,0:T(8,128)S(1)} collective-permute-done((f32[16,1024]{1,0:T(8,128)S(1)}, f32[16,1024]{1,0:T(8,128)S(1)}, u32[]{:S(2)}, u32[]{:S(2)}) %collective-permute-start.6) | collective-permute-done | bytes 65568 | tf_op jit(solution)/shard_map/ppermute | solution.py:62
  21.6 0.5 %collective-permute-done.7.refs_3_ = f32[16,1024]{1,0:T(8,128)S(1)} collective-permute-done((f32[16,1024]{1,0:T(8,128)S(1)}, f32[16,1024]{1,0:T(8,128)S(1)}, u32[]{:S(2)}, u32[]{:S(2)}) %collective-permute-start.7) | collective-permute-done | bytes 65568 | tf_op jit(solution)/shard_map/ppermute | solution.py:62
  22.1 0.1 shard_map.129
  22.2 1.3 %collective-permute-start.10 = (f32[16,1024]{1,0:T(8,128)S(1)}, f32[16,1024]{1,0:T(8,128)S(1)}, u32[]{:S(2)}, u32[]{:S(2)}) collective-permute-start(f32[16,1024]{1,0:T(8,128)S(1)} %get-tuple-element.35.mine), channel_id=1, source_target_pairs={{0,8},{4,12},{8,0},{12,4},{16,24},{20,28},{24,16},{28,20},{1,9},{5... | collective-permute-start | bytes 196616 | tf_op jit(solution)/shard_map/ppermute | solution.py:58
  23.5 0.0 collective-permute-start.12
  23.5 1.6 %collective-permute-start.8 = (f32[16,1024]{1,0:T(8,128)S(1)}, f32[16,1024]{1,0:T(8,128)S(1)}, u32[]{:S(2)}, u32[]{:S(2)}) collective-permute-start(f32[16,1024]{1,0:T(8,128)S(1)} %get-tuple-element.35.mine), channel_id=1, source_target_pairs={{0,24},{4,28},{8,16},{12,20},{16,8},{20,12},{24,0},{28,4},{1,25},{... | collective-permute-start | bytes 196616 | tf_op jit(solution)/shard_map/ppermute | solution.py:58
  25.0 1.4 %collective-permute-start.14 = (f32[16,1024]{1,0:T(8,128)S(1)}, f32[16,1024]{1,0:T(8,128)S(1)}, u32[]{:S(2)}, u32[]{:S(2)}) collective-permute-start(f32[16,1024]{1,0:T(8,128)S(1)} %get-tuple-element.35.mine), channel_id=1, source_target_pairs={{0,4},{4,0},{8,12},{12,8},{16,20},{20,16},{24,28},{28,24},{1,5},{5... | collective-permute-start | bytes 196616 | tf_op jit(solution)/shard_map/ppermute | solution.py:48
  26.5 0.0 collective-permute-done.10.refs_0_
  26.5 0.0 collective-permute-start.11
  26.5 4.9 %collective-permute-done.12.refs_2_ = f32[16,1024]{1,0:T(8,128)S(1)} collective-permute-done((f32[16,1024]{1,0:T(8,128)S(1)}, f32[16,1024]{1,0:T(8,128)S(1)}, u32[]{:S(2)}, u32[]{:S(2)}) %collective-permute-start.12) | collective-permute-done | bytes 65568 | tf_op jit(solution)/shard_map/ppermute | solution.py:58
  31.4 0.0 collective-permute-start.13
  31.4 0.0 collective-permute-done.8.refs_4_
  31.4 0.5 %collective-permute-start.9 = (f32[16,1024]{1,0:T(8,128)S(1)}, f32[16,1024]{1,0:T(8,128)S(1)}, u32[]{:S(2)}, u32[]{:S(2)}) collective-permute-start(f32[16,1024]{1,0:T(8,128)S(1)} %collective-permute-done.8.refs_4_), channel_id=1, source_target_pairs={{0,4},{4,0},{8,12},{12,8},{16,20},{20,16},{24,28},{28,24},{1,5},{5... | collective-permute-start | bytes 196616 | tf_op jit(solution)/shard_map/ppermute | solution.py:48
  32.0 0.8 %shard_map.133 = (f32[1,1,128,1024]{3,2,1,0:T(8,128)}, f32[1,16,1024]{2,1,0:T(8,128)}, f32[1,16,1024]{2,1,0:T(8,128)}) custom-call(f32[1,1,128,1024]{3,2,1,0:T(8,128)S(1)} %bitcast.15, f32[1,16,1024]{2,1,0:T(8,128)S(1)} %bitcast.16, f32[1,16,1024]{2,1,0:T(8,128)S(1)} %bitcast.17), custom_call_target="tpu_custom_call" | custom-call | tf_op jit(solution)/shard_map/pallas_call | solution.py:185
  32.8 0.0 collective-permute-done.14.given
  32.8 0.0 copy-done.1
  32.8 0.0 copy-done
  32.8 0.8 %shard_map.130 = (f32[128,1024]{1,0:T(8,128)}, f32[128,1024]{1,0:T(8,128)}, f32[4,1024]{1,0:T(4,128)}) custom-call(f32[16,1024]{1,0:T(8,128)S(1)} %get-tuple-element.35.mine, f32[16,1024]{1,0:T(8,128)S(1)} %collective-permute-done.14.given, f32[128,1024]{1,0:T(8,128)S(1)} %copy-done, f32[128,1024]{1,0:T(8,128)S(1)} %copy-done.1, ...), custom_call_target="tpu_custom_call" | custom-call | tf_op jit(solution)/shard_map/pallas_call | solution.py:270
  33.6 0.0 collective-permute-done.11.refs_1_
  33.6 0.0 collective-permute-done.13.refs_3_
  33.6 1.0 %shard_map.131 = (f32[128,1024]{1,0:T(8,128)}, f32[128,1024]{1,0:T(8,128)}) custom-call(f32[16,1024]{1,0:T(8,128)S(1)} %collective-permute-done.10.refs_0_, f32[16,1024]{1,0:T(8,128)S(1)} %collective-permute-done.11.refs_1_, f32[16,1024]{1,0:T(8,128)S(1)} %collective-permute-done.12.refs_2_, ...), custom_call_target="tpu_custom_call", output_to_operand_aliasing={{0}: (7, {}), {1}: (8, {})} | custom-call | tf_op jit(solution)/shard_map/pallas_call | solution.py:245
  34.6 0.0 collective-permute-done.9.refs_0_
  34.6 0.7 %shard_map.132 = (f32[128,1024]{1,0:T(8,128)}, f32[128,1024]{1,0:T(8,128)}) custom-call(f32[16,1024]{1,0:T(8,128)S(1)} %collective-permute-done.9.refs_0_, f32[128,1024]{1,0:T(8,128)S(1)} %copy-done, f32[128,1024]{1,0:T(8,128)S(1)} %copy-done.1, f32[128,1024]{1,0:T(8,128)} %get-tuple-element.39.refs_3_, ...), custom_call_target="tpu_custom_call", output_to_operand_aliasing={{0}: (3, {}), {1}: (4, {})} | custom-call | tf_op jit(solution)/shard_map/pallas_call | solution.py:245
  (3 shorter events, 0.0 us)
Async XLA Ops:
  2.2 6.6 %collective-permute-start = (f32[3,16,1024]{2,1,0:T(8,128)S(1)}, f32[3,16,1024]{2,1,0:T(8,128)S(1)}, u32[]{:S(2)}, u32[]{:S(2)}) collective-permute-start(f32[3,16,1024]{2,1,0:T(8,128)S(1)} %get-tuple-element.29), channel_id=1, source_target_pairs={{0,4},{4,0},{8,12},{12,8},{16,20},{20,16},{24,28},{28,24},{1,5},{5... | collective-permute-start | bytes 589832 | tf_op jit(solution)/shard_map/ppermute | solution.py:48
  2.7 1.3 %collective-permute-start.1 = (f32[16,1024]{1,0:T(8,128)S(1)}, f32[16,1024]{1,0:T(8,128)S(1)}, u32[]{:S(2)}, u32[]{:S(2)}) collective-permute-start(f32[16,1024]{1,0:T(8,128)S(1)} %get-tuple-element.31), channel_id=1, source_target_pairs={{0,4},{4,0},{8,12},{12,8},{16,20},{20,16},{24,28},{28,24},{1,5},{5... | collective-permute-start | bytes 196616 | tf_op jit(solution)/shard_map/ppermute | solution.py:48
  4.0 7.3 %collective-permute-start.2 = (f32[16,1024]{1,0:T(8,128)S(1)}, f32[16,1024]{1,0:T(8,128)S(1)}, u32[]{:S(2)}, u32[]{:S(2)}) collective-permute-start(f32[16,1024]{1,0:T(8,128)S(1)} %add.9), channel_id=1, source_target_pairs={{0,28},{4,24},{8,20},{12,16},{16,12},{20,8},{24,4},{28,0},{1,29},{... | collective-permute-start | bytes 196616 | tf_op jit(solution)/shard_map/ppermute | solution.py:58
  8.8 5.8 %copy-start.4 = (f32[4,1024]{1,0:T(4,128)S(1)}, f32[4,1024]{1,0:T(4,128)}, u32[]{:S(2)}) copy-start(f32[4,1024]{1,0:T(4,128)} %refs_7_.1) | copy-start | bytes 49156
  8.8 5.7 %collective-permute-start.3 = (f32[16,1024]{1,0:T(8,128)S(1)}, f32[16,1024]{1,0:T(8,128)S(1)}, u32[]{:S(2)}, u32[]{:S(2)}) collective-permute-start(f32[16,1024]{1,0:T(8,128)S(1)} %get-tuple-element.51), channel_id=1, source_target_pairs={{0,20},{4,16},{8,28},{12,24},{16,4},{20,0},{24,12},{28,8},{1,21},{... | collective-permute-start | bytes 196616 | tf_op jit(solution)/shard_map/ppermute | solution.py:58
  8.9 5.7 %copy-start.2 = (f32[1,16,1024]{2,1,0:T(8,128)S(1)}, f32[1,16,1024]{2,1,0:T(8,128)}, u32[]{:S(2)}) copy-start(f32[1,16,1024]{2,1,0:T(8,128)} %param.13) | copy-start | bytes 196612
  8.9 5.7 %copy-start.3 = (f32[1,16,1024]{2,1,0:T(8,128)S(1)}, f32[1,16,1024]{2,1,0:T(8,128)}, u32[]{:S(2)}) copy-start(f32[1,16,1024]{2,1,0:T(8,128)} %param.14) | copy-start | bytes 196612
  8.9 5.6 %collective-permute-start.4 = (f32[16,1024]{1,0:T(8,128)S(1)}, f32[16,1024]{1,0:T(8,128)S(1)}, u32[]{:S(2)}, u32[]{:S(2)}) collective-permute-start(f32[16,1024]{1,0:T(8,128)S(1)} %get-tuple-element.50), channel_id=1, source_target_pairs={{0,12},{4,8},{8,4},{12,0},{16,28},{20,24},{24,20},{28,16},{1,13},{... | collective-permute-start | bytes 196616 | tf_op jit(solution)/shard_map/ppermute | solution.py:58
  14.6 18.3 %copy-start.1 = (f32[128,1024]{1,0:T(8,128)S(1)}, f32[128,1024]{1,0:T(8,128)}, u32[]{:S(2)}) copy-start(f32[128,1024]{1,0:T(8,128)} %refs_2_.1) | copy-start | bytes 1572868
  14.8 18.1 %copy-start = (f32[128,1024]{1,0:T(8,128)S(1)}, f32[128,1024]{1,0:T(8,128)}, u32[]{:S(2)}) copy-start(f32[128,1024]{1,0:T(8,128)} %refs_1_.1) | copy-start | bytes 1572868
  14.8 5.2 %collective-permute-start.5 = (f32[16,1024]{1,0:T(8,128)S(1)}, f32[16,1024]{1,0:T(8,128)S(1)}, u32[]{:S(2)}, u32[]{:S(2)}) collective-permute-start(f32[16,1024]{1,0:T(8,128)S(1)} %get-tuple-element.34.refs_0_), channel_id=1, source_target_pairs={{0,3},{1,2},{2,1},{3,0},{4,7},{5,6},{6,5},{7,4},{8,11},{9,10},{10,... | collective-permute-start | bytes 196616 | tf_op jit(solution)/shard_map/ppermute | solution.py:62
  17.3 4.3 %collective-permute-start.6 = (f32[16,1024]{1,0:T(8,128)S(1)}, f32[16,1024]{1,0:T(8,128)S(1)}, u32[]{:S(2)}, u32[]{:S(2)}) collective-permute-start(f32[16,1024]{1,0:T(8,128)S(1)} %get-tuple-element.34.refs_0_), channel_id=1, source_target_pairs={{0,2},{1,3},{2,0},{3,1},{4,6},{5,7},{6,4},{7,5},{8,10},{9,11},{10,... | collective-permute-start | bytes 196616 | tf_op jit(solution)/shard_map/ppermute | solution.py:62
  17.8 4.3 %collective-permute-start.7 = (f32[16,1024]{1,0:T(8,128)S(1)}, f32[16,1024]{1,0:T(8,128)S(1)}, u32[]{:S(2)}, u32[]{:S(2)}) collective-permute-start(f32[16,1024]{1,0:T(8,128)S(1)} %get-tuple-element.34.refs_0_), channel_id=1, source_target_pairs={{0,1},{1,0},{2,3},{3,2},{4,5},{5,4},{6,7},{7,6},{8,9},{9,8},{10,11... | collective-permute-start | bytes 196616 | tf_op jit(solution)/shard_map/ppermute | solution.py:62
  22.2 4.3 %collective-permute-start.10 = (f32[16,1024]{1,0:T(8,128)S(1)}, f32[16,1024]{1,0:T(8,128)S(1)}, u32[]{:S(2)}, u32[]{:S(2)}) collective-permute-start(f32[16,1024]{1,0:T(8,128)S(1)} %get-tuple-element.35.mine), channel_id=1, source_target_pairs={{0,8},{4,12},{8,0},{12,4},{16,24},{20,28},{24,16},{28,20},{1,9},{5... | collective-permute-start | bytes 196616 | tf_op jit(solution)/shard_map/ppermute | solution.py:58
  23.5 8.0 %collective-permute-start.12 = (f32[16,1024]{1,0:T(8,128)S(1)}, f32[16,1024]{1,0:T(8,128)S(1)}, u32[]{:S(2)}, u32[]{:S(2)}) collective-permute-start(f32[16,1024]{1,0:T(8,128)S(1)} %get-tuple-element.35.mine), channel_id=1, source_target_pairs={{0,20},{4,16},{8,28},{12,24},{16,4},{20,0},{24,12},{28,8},{1,21},{... | collective-permute-start | bytes 196616 | tf_op jit(solution)/shard_map/ppermute | solution.py:58
  23.5 8.0 %collective-permute-start.8 = (f32[16,1024]{1,0:T(8,128)S(1)}, f32[16,1024]{1,0:T(8,128)S(1)}, u32[]{:S(2)}, u32[]{:S(2)}) collective-permute-start(f32[16,1024]{1,0:T(8,128)S(1)} %get-tuple-element.35.mine), channel_id=1, source_target_pairs={{0,24},{4,28},{8,16},{12,20},{16,8},{20,12},{24,0},{28,4},{1,25},{... | collective-permute-start | bytes 196616 | tf_op jit(solution)/shard_map/ppermute | solution.py:58
  25.0 7.8 %collective-permute-start.14 = (f32[16,1024]{1,0:T(8,128)S(1)}, f32[16,1024]{1,0:T(8,128)S(1)}, u32[]{:S(2)}, u32[]{:S(2)}) collective-permute-start(f32[16,1024]{1,0:T(8,128)S(1)} %get-tuple-element.35.mine), channel_id=1, source_target_pairs={{0,4},{4,0},{8,12},{12,8},{16,20},{20,16},{24,28},{28,24},{1,5},{5... | collective-permute-start | bytes 196616 | tf_op jit(solution)/shard_map/ppermute | solution.py:48
  26.5 7.1 %collective-permute-start.11 = (f32[16,1024]{1,0:T(8,128)S(1)}, f32[16,1024]{1,0:T(8,128)S(1)}, u32[]{:S(2)}, u32[]{:S(2)}) collective-permute-start(f32[16,1024]{1,0:T(8,128)S(1)} %collective-permute-done.10.refs_0_), channel_id=1, source_target_pairs={{0,4},{4,0},{8,12},{12,8},{16,20},{20,16},{24,28},{28,24},{1,5},{5... | collective-permute-start | bytes 196616 | tf_op jit(solution)/shard_map/ppermute | solution.py:48
  31.4 2.2 %collective-permute-start.13 = (f32[16,1024]{1,0:T(8,128)S(1)}, f32[16,1024]{1,0:T(8,128)S(1)}, u32[]{:S(2)}, u32[]{:S(2)}) collective-permute-start(f32[16,1024]{1,0:T(8,128)S(1)} %collective-permute-done.12.refs_2_), channel_id=1, source_target_pairs={{0,4},{4,0},{8,12},{12,8},{16,20},{20,16},{24,28},{28,24},{1,5},{5... | collective-permute-start | bytes 196616 | tf_op jit(solution)/shard_map/ppermute | solution.py:48
  31.4 3.2 %collective-permute-start.9 = (f32[16,1024]{1,0:T(8,128)S(1)}, f32[16,1024]{1,0:T(8,128)S(1)}, u32[]{:S(2)}, u32[]{:S(2)}) collective-permute-start(f32[16,1024]{1,0:T(8,128)S(1)} %collective-permute-done.8.refs_4_), channel_id=1, source_target_pairs={{0,4},{4,0},{8,12},{12,8},{16,20},{20,16},{24,28},{28,24},{1,5},{5... | collective-permute-start | bytes 196616 | tf_op jit(solution)/shard_map/ppermute | solution.py:48
